TPU v7x, 32 devices: a whole 2x2x4 slice. The times are simulated.
32 devices in a mesh: groups: 2 (over y), seq: 4 (over z), head: 4 (over x, core).
Axes of the slice: x: 2, y: 2, z: 4, core: 2. Of those that a mesh axis runs over, the one named last changes fastest.
Arguments:
- queries: bfloat16 [32, 3, 32, 128], P('groups', None, 'head'), parts along dimension 0, may hold values from -8 to 8
- new_kv: bfloat16 [4, 16, 3, 4, 128], P('groups', None, None, 'head'), parts along dimension 0, may hold values from -16 to 16
- res_kv: bfloat16 [4, 2, 16384, 4, 128], P('groups', None, 'seq', 'head'), parts along dimension 0, may hold values from -16 to 16
- prefill_kv: bfloat16 [4, 4, 4096, 128], P('groups', None, ('seq', 'head')), parts along dimension 0, may hold values from -16 to 16
- block_table: int32 [128], P('groups'), parts along dimension 0, may hold values from 0 to 63, as said below
- lengths: int32 [6], P('groups'), parts along dimension 0, may hold values from 4096 to 16384, as said below
- join_step: int32 [2], P('groups'), parts along dimension 0, may hold values from 1 to 15
Outputs:
- attn_out: bfloat16 [32, 3, 32, 128], P('groups', None, 'head'), parts along dimension 0
- new_cache: bfloat16 [4, 4, 4096, 128], P('groups', 'head', 'seq'), parts along dimension 0
There are 2 independent parts, one for each index of `groups`. A program takes and returns all parts, laid end to end along the dimension named above; each array names one. Nothing has to cross between parts.
Inputs may be any that keep to these rules, and one draw needn't show every extreme that they name: `block_table`: A permutation of 0 to 63. In each aligned run of 4 entries (the blocks of one prefill device) every aligned range of 16 slots is named exactly 1 times. `lengths`: entries 0 to 1 lie between 4096 and 16384, and one of them equals 16384; entry 2 equals 4096.
All inputs are finite; a program needn't handle non-finite values.
Results may differ from a plain program's by a relative error of at most 0.0039.
Values may be sent and summed in bfloat16 or wider, within the bound.
A program may use at most 64 MiB of HBM per device.

v0:
```python
import math

import jax
import jax.numpy as jnp
from jax import lax
from jax.sharding import PartitionSpec as P

very_low = -1e30


def merged_2(shard, axis, combine):
    everything = jax.tree.map(lambda part: lax.all_gather(part, axis), shard)
    initial = jax.tree.map(lambda part: part[0], everything)

    def lap(k, so_far):
        return combine(so_far, jax.tree.map(lambda part: part[k], everything))

    return lax.fori_loop(1, lax.axis_size(axis), lap, initial)


def partial_softmax(query_rows, key_rows, value_rows, valid_mask, score_scale):
    scores = (
        jnp.einsum("rd,pd->rp", query_rows, key_rows, preferred_element_type=jnp.float32)
        * score_scale
    )
    scores = jnp.where(valid_mask[None, :], scores, very_low)
    row_max = jnp.max(scores, axis=-1)
    weights = jnp.where(valid_mask[None, :], jnp.exp(scores - row_max[:, None]), 0.0)
    row_total = jnp.sum(weights, axis=-1)
    summed = jnp.einsum(
        "rp,pd->rd", weights.astype(jnp.bfloat16), value_rows, preferred_element_type=jnp.float32
    )
    return (row_max, row_total, summed)


def combine(earlier_part, later_part):
    joint_max = jnp.maximum(earlier_part[0], later_part[0])
    left_scale = jnp.exp(earlier_part[0] - joint_max)
    right_scale = jnp.exp(later_part[0] - joint_max)
    return (
        joint_max,
        earlier_part[1] * left_scale + later_part[1] * right_scale,
        earlier_part[2] * left_scale[..., None] + later_part[2] * right_scale[..., None],
    )


def per_device(queries, new_kv, res_kv, prefill_kv, block_table, lengths, join_step):
    seq_index = lax.axis_index("seq")
    head_index = lax.axis_index("head")
    seq_count = lax.axis_size("seq")
    head_count = lax.axis_size("head")
    senders = seq_count * head_count
    step_count, request_count, group_size, head_dim = queries.shape
    resident = res_kv.shape[1]
    res_rows = res_kv.shape[2]
    score_scale = 1.0 / math.sqrt(head_dim)
    joined = join_step[0]
    head_total = prefill_kv.shape[1]
    new_rows = prefill_kv.shape[2]
    total_blocks = block_table.shape[0]
    dev_blocks = total_blocks // senders
    block_len = new_rows // dev_blocks
    page_count = dev_blocks // seq_count
    slot_count = page_count * senders
    table_rows = block_table.reshape(senders, dev_blocks)
    sender = seq_index * head_count + head_index
    own_slots = lax.dynamic_slice_in_dim(table_rows, sender, 1, 0)[0]
    send_order = jnp.argsort(own_slots)
    blocks = prefill_kv.reshape(2, head_total, dev_blocks, block_len, head_dim)
    ordered = jnp.take(blocks, send_order, axis=2)
    sender_ids = jnp.arange(senders, dtype=jnp.int32)
    outgoing = jnp.swapaxes(ordered, 1, 2).reshape(2, senders, page_count * block_len, head_dim)
    arrived = lax.all_to_all(outgoing, ("seq", "head"), split_axis=1, concat_axis=1, tiled=True)
    inverse = (
        jnp.zeros((total_blocks,), jnp.int32)
        .at[block_table]
        .set(jnp.arange(total_blocks, dtype=jnp.int32))
    )
    rank_within = jnp.argsort(jnp.argsort(table_rows, axis=1), axis=1).reshape(-1)
    held_blocks = lax.dynamic_slice_in_dim(inverse, seq_index * slot_count, slot_count, 0)
    page_index = rank_within[held_blocks] - seq_index * page_count
    take_rows = sender_ids[held_blocks // dev_blocks] * page_count + page_index
    relaid = jnp.take(arrived, take_rows, axis=1)
    new_cache = relaid.reshape(2, 1, slot_count * block_len, head_dim)
    positions = (
        held_blocks[:, None] * block_len + jnp.arange(block_len, dtype=jnp.int32)[None, :]
    ).reshape(-1)
    partials = []
    res_positions = seq_index * res_rows + jnp.arange(res_rows, dtype=jnp.int32)
    for request in range(resident):
        query_rows = queries[:, request].reshape(step_count * group_size, head_dim)
        partials.append(
            partial_softmax(
                query_rows,
                res_kv[0, request, :, 0],
                res_kv[1, request, :, 0],
                res_positions < lengths[request],
                score_scale,
            )
        )
    query_rows = queries[:, resident].reshape(step_count * group_size, head_dim)
    partials.append(
        partial_softmax(
            query_rows, new_cache[0, 0], new_cache[1, 0], positions < lengths[resident], score_scale
        )
    )
    stacked_max = jnp.stack([member[0] for member in partials])
    stacked_total = jnp.stack([member[1] for member in partials])
    stacked_sum = jnp.stack([member[2] for member in partials])
    merged = merged_2((stacked_max, stacked_total, stacked_sum), "seq", combine)
    row_max = jnp.transpose(merged[0].reshape(request_count, step_count, group_size), (1, 0, 2))
    row_total = jnp.transpose(merged[1].reshape(request_count, step_count, group_size), (1, 0, 2))
    summed = jnp.transpose(
        merged[2].reshape(request_count, step_count, group_size, head_dim), (1, 0, 2, 3)
    )
    fresh_keys = new_kv[0, :, :, 0]
    fresh_values = new_kv[1, :, :, 0]
    fresh_scores = (
        jnp.einsum("trqd,urd->trqu", queries, fresh_keys, preferred_element_type=jnp.float32)
        * score_scale
    )
    step_ids = jnp.arange(step_count, dtype=jnp.int32)
    request_ids = jnp.arange(request_count, dtype=jnp.int32)
    allowed = (step_ids[None, None, :] <= step_ids[:, None, None]) & (
        (request_ids[None, :, None] < resident) | (step_ids[None, None, :] >= joined)
    )
    fresh_scores = jnp.where(allowed[:, :, None, :], fresh_scores, very_low)
    joint_max = jnp.maximum(row_max, jnp.max(fresh_scores, axis=-1))
    rescale = jnp.exp(row_max - joint_max)
    fresh_weight = jnp.where(
        allowed[:, :, None, :], jnp.exp(fresh_scores - joint_max[..., None]), 0.0
    )
    row_total = row_total * rescale + jnp.sum(fresh_weight, axis=-1)
    summed = summed * rescale[..., None] + jnp.einsum(
        "trqu,urd->trqd",
        fresh_weight.astype(jnp.bfloat16),
        fresh_values,
        preferred_element_type=jnp.float32,
    )
    result = summed / row_total[..., None]
    live_rows = (request_ids[None, :] < resident) | (step_ids[:, None] >= joined)
    attn_out = jnp.where(live_rows[:, :, None, None], result, 0.0).astype(jnp.bfloat16)
    return (attn_out, new_cache)


def solution(mesh):
    in_specs = (
        P("groups", None, "head", None),
        P("groups", None, None, "head", None),
        P("groups", None, "seq", "head", None),
        P("groups", None, ("seq", "head"), None),
        P("groups"),
        P("groups"),
        P("groups"),
    )
    out_specs = (P("groups", None, "head", None), P("groups", "head", "seq", None))
    return jax.shard_map(
        per_device, mesh=mesh, in_specs=in_specs, out_specs=out_specs, check_vma=False
    )
```

profile of v0, /device:TPU:0, one launch (start us, length us, event | category | flops | bytes accessed | tf_op | source)
XLA Modules:
  0.0 72.9 jit_solution(4330611319050637501)
XLA Ops:
  0.7 0.8 %reshape.206 = s32[16,4]{1,0:T(8,128)S(1)} reshape(s32[64]{0:T(128)} %param.13) | data formatting | bytes 512 | tf_op jit(solution)/shard_map/reshape | solution.py:65
  1.5 0.7 %sort.50 = (s32[4]{0:T(128)}, s32[4]{0:T(128)S(1)}) sort(s32[4]{0:T(128)S(1)} %dynamic-slice_bitcast_fusion, s32[4]{0:T(128)S(1)} %iota.68), dimensions={0}, to_apply=%region_5.6 | sort | flops 8 | bytes 64 | tf_op jit(solution)/shard_map/jit(argsort)/sort | solution.py:68
  2.3 0.6 gather_fusion.2
  2.9 0.1 select_bitcast_fusion
  3.1 0.8 %copy.40 = bf16[2,16,64,128]{3,2,0,1:T(8,128)(2,1)} copy(bf16[2,16,64,128]{3,2,1,0:T(8,128)(2,1)S(1)} %bitcast.150) | data formatting | bytes 1048576 | tf_op jit(solution)/shard_map/reshape | solution.py:72
  3.9 7.4 %all-to-all-start = ((bf16[2,16,64,128]{3,2,0,1:T(8,128)(2,1)}), bf16[2,16,64,128]{3,2,0,1:T(8,128)(2,1)S(1)}, u32[]{:S(2)}, u32[]{:S(2)}) async-start(bf16[2,16,64,128]{3,2,0,1:T(8,128)(2,1)} %copy.40), calls=%async_computation | async-start | bytes 1048576 | tf_op jit(solution)/shard_map/all_to_all | solution.py:73
  11.4 0.1 copy.37
  11.5 0.6 sort.48
  12.1 0.6 sort.49
  12.7 0.1 copy.38
  12.8 0.1 reshape.207
  12.9 0.8 %scatter_custom_fusion = s32[64]{0:T(128)S(1)} fusion(s32[64]{0:T(128)S(1)} %compare_select_fusion.4, s32[64]{0:T(128)S(1)} %iota.64, s32[]{:T(128)} %constant.95.clone.1), kind=kCustom, calls=%fused_computation.112 | custom fusion | bytes 260 | tf_op jit(solution)/shard_map/scatter | solution.py:77
  13.7 0.1 broadcast_multiply_fusion
  13.8 0.7 gather_fusion.1
  14.4 0.7 gather_fusion
  15.8 0.6 fusion.60
  16.4 0.6 add_compare_fusion
  17.1 0.1 lt.109
  17.2 0.1 broadcast_in_dim.168
  17.3 1.3 %fusion.47 = (pred[4096]{0:T(1024)(128)(4,1)S(1)}, pred[4096]{0:T(1024)(128)(4,1)S(1)}) fusion(s32[]{:T(128)} %bitcast.8, s32[]{:T(128)S(6)} %mul.118, s32[]{:T(128)} %bitcast.4), kind=kLoop, calls=%fused_computation.72 | loop fusion | flops 12288 | bytes 8204 | tf_op jit(solution)/shard_map/lt | solution.py:97
  18.6 1.7 %fusion.63 = (f32[128]{0:T(128)S(1)}, f32[128,4096]{1,0:T(8,128)S(1)}) fusion(bf16[2,2,4096,1,128]{4,2,3,1,0:T(8,128)(2,1)} %param.11, bf16[16,3,8,128]{3,2,1,0:T(8,128)(2,1)S(1)} %copy-done.2, pred[4096]{0:T(1024)(128)(4,1)S(1)} %get-tuple-element.237), kind=kOutput, calls=%fused_computation.121 | convolution fusion | flops 135790464 | bytes 3183104 | tf_op jit(solution)/shard_map/rd,pd->rp/dot_general | solution.py:23
  20.4 1.8 %fusion.64 = (f32[128]{0:T(128)S(1)}, f32[128,4096]{1,0:T(8,128)S(1)}) fusion(bf16[2,2,4096,1,128]{4,2,3,1,0:T(8,128)(2,1)} %param.11, bf16[16,3,8,128]{3,2,1,0:T(8,128)(2,1)S(1)} %copy-done.2, pred[4096]{0:T(1024)(128)(4,1)S(1)} %get-tuple-element.238), kind=kOutput, calls=%fused_computation.122 | convolution fusion | flops 135790464 | bytes 3183104 | tf_op jit(solution)/shard_map/rd,pd->rp/dot_general | solution.py:23
  22.2 0.1 broadcast_and_fusion
  22.3 0.5 fusion.8
  22.8 0.5 fusion.6
  23.4 0.4 fusion.61
  23.8 0.7 copy-done.1
  24.5 0.5 convolution_bitcast_fusion.1
  25.0 0.5 convolution_bitcast_fusion.2
  25.6 0.6 gather_fusion.3
  26.3 0.1 broadcast_select_fusion
  26.5 0.3 fusion.62
  26.8 0.2 fusion.32
  27.0 0.5 convolution_bitcast_fusion.3
  27.5 12.4 %all-gather.3 = f32[4,3,128]{2,1,0:T(4,128)S(1)} all-gather(f32[1,3,128]{2,1,0:T(4,128)S(1)} %maximum_bitcast_fusion), channel_id=2, replica_groups=mesh['groups'=2,'seq'=4,'head'=4] {'seq'}, dimensions={0}, use_global_device_ids=true | all-gather | bytes 7680 | tf_op jit(solution)/shard_map/all_gather | solution.py:12
  39.9 11.9 %all-gather.4 = f32[4,3,128]{2,1,0:T(4,128)S(1)} all-gather(f32[1,3,128]{2,1,0:T(4,128)S(1)} %maximum_bitcast_fusion.1), channel_id=3, replica_groups=mesh['groups'=2,'seq'=4,'head'=4] {'seq'}, dimensions={0}, use_global_device_ids=true | all-gather | bytes 7680 | tf_op jit(solution)/shard_map/all_gather | solution.py:12
  51.9 17.6 %all-gather.2 = f32[12,128,128]{2,1,0:T(8,128)S(1)} all-gather(f32[3,128,128]{2,1,0:T(8,128)S(1)} %pad_maximum_fusion), channel_id=4, replica_groups=mesh['groups'=2,'seq'=4,'head'=4] {'seq'}, dimensions={0}, use_global_device_ids=true | all-gather | bytes 983040 | tf_op jit(solution)/shard_map/all_gather | solution.py:12
  69.5 0.8 %while.19 = (s32[]{:T(128)}, f32[3,128]{1,0:T(4,128)S(1)}, f32[3,128]{1,0:T(4,128)S(1)}, f32[3,128,128]{2,1,0:T(8,128)S(1)}, f32[4,3,128]{2,1,0:T(4,128)S(1)}, /...) while((s32[]{:T(128)}, f32[3,128]{1,0:T(4,128)S(1)}, ...), condition=%wide.region_11.12_spmd, body=%wide.region_10.11_spmd.sunk | while | flops 149765 | bytes 605327 | solution.py:18
  69.5 0.2 fusion.71
  69.8 0.2 fusion.71
  70.0 0.2 fusion.71
  70.3 0.1 reshape.211
  70.4 0.1 reshape.212
  70.6 0.1 fusion.38
  70.9 0.1 copy.47
  71.0 0.2 fusion.15
  71.2 0.7 copy.51
  71.9 1.0 %bitcast_select_fusion = bf16[2,1,1024,128]{3,2,0,1:T(8,128)(2,1)} fusion(bf16[2,16,64,128]{3,2,1,0:T(8,128)(2,1)S(1)} %copy.50, pred[1024]{0:T(1024)(128)(4,1)S(1)} %broadcast_in_dim.168), kind=kLoop, calls=%fused_computation.50 | loop fusion | flops 262144 | bytes 1049600 | tf_op jit(solution)/shard_map/jit(_take)/select_n | solution.py:83
  (51 shorter events, 1.0 us)
Async XLA Ops:
  0.6 1.6 %copy-start = (bf16[2,4,256,128]{3,2,1,0:T(8,128)(2,1)S(1)}, bf16[2,4,256,128]{3,2,1,0:T(8,128)(2,1)}, u32[]{:S(2)}) copy-start(bf16[2,4,256,128]{3,2,1,0:T(8,128)(2,1)} %param.12) | copy-start | bytes 1572868
  2.9 8.4 %copy-start.5 = (s32[64]{0:T(128)S(1)}, s32[64]{0:T(128)}, u32[]{:S(2)}) copy-start(s32[64]{0:T(128)} %param.13) | copy-start | bytes 772
  3.0 12.8 %copy-start.4 = (s32[3]{0:T(128)S(1)}, s32[3]{0:T(128)}, u32[]{:S(2)}) copy-start(s32[3]{0:T(128)} %param.14) | copy-start | bytes 40
  3.1 15.6 %copy-start.2 = (bf16[16,3,8,128]{3,2,1,0:T(8,128)(2,1)S(1)}, bf16[16,3,8,128]{3,2,1,0:T(8,128)(2,1)}, u32[]{:S(2)}) copy-start(bf16[16,3,8,128]{3,2,1,0:T(8,128)(2,1)} %param.9) | copy-start | bytes 294916
  3.9 21.7 %all-to-all-start = ((bf16[2,16,64,128]{3,2,0,1:T(8,128)(2,1)}), bf16[2,16,64,128]{3,2,0,1:T(8,128)(2,1)S(1)}, u32[]{:S(2)}, u32[]{:S(2)}) async-start(bf16[2,16,64,128]{3,2,0,1:T(8,128)(2,1)} %copy.40), calls=%async_computation | async-start | bytes 1048576 | tf_op jit(solution)/shard_map/all_to_all | solution.py:73
  22.3 1.2 %copy-start.3 = (bf16[2,16,3,1,128]{4,1,3,2,0:T(8,128)(2,1)S(1)}, bf16[2,16,3,1,128]{4,1,3,2,0:T(8,128)(2,1)}, u32[]{:S(2)}) copy-start(bf16[2,16,3,1,128]{4,1,3,2,0:T(8,128)(2,1)} %param.10) | copy-start | bytes 73732
  22.3 2.2 %copy-start.1 = (bf16[2,2,4096,1,128]{4,2,3,1,0:T(8,128)(2,1)S(1)}, bf16[2,2,4096,1,128]{4,2,3,1,0:T(8,128)(2,1)}, u32[]{:S(2)}) copy-start(bf16[2,2,4096,1,128]{4,2,3,1,0:T(8,128)(2,1)} %param.11) | copy-start | bytes 12582916
where the time goes:
time: 73.3 us; the launch traced here: 72.9 us
  blocking collectives  41.9 us (57%)
  local copies, waits for them, and re-layouts  8.28 us (11%)
  other arithmetic  7.65 us (10%)
  starting transfers between devices  7.39 us (10%)
  matrix products  5.95 us (8%)
  between operations  1.63 us (2%)
    all_gather x3, blocking collectives, merged_2(): everything = jax.tree.map(lambda part: lax.all_gather(part, axis), shard)  41.9 us
    all_to_all x1, starting transfers between devices, per_device(): lax.all_to_all(outgoing, ('seq', 'head'), split_axis=1, concat_axis=1, ti...  7.39 us
    dot_general x3, matrix products, partial_softmax(): jnp.einsum('rd,pd->rp', query_rows, key_rows, preferred_element_type=jnp....  3.83 us
    dot_general x3, matrix products, partial_softmax(): jnp.einsum('rp,pd->rd', weights.astype(jnp.bfloat16), value_rows, preferr...  1.52 us
  transfers between devices with their start and end apart: 1, of which 0 were waited for; matrix products, arithmetic and copies ran while one was open for 17% of the time, Pallas kernels for 0%

commit v1 on v0

v1 whole, which is shorter than its diff:
```python
import functools
import math

import jax
import jax.numpy as jnp
from jax import lax
from jax.experimental import pallas as pl
from jax.experimental.pallas import tpu as pltpu
from jax.sharding import PartitionSpec as P

very_low = -1e30
MESH = pl.DeviceIdType.MESH
NT = (((1,), (1,)), ((), ()))
TN = (((0,), (0,)), ((), ()))


def kernel(
    seq_count,
    head_count,
    queries,
    fresh,
    prefill,
    table,
    lengths,
    join_step,
    res_kv,
    attn_out,
    new_cache,
    res_buf,
    staged,
    arrived,
    own_acc,
    own_stat,
    fresh_acc,
    fresh_stat,
    out_acc,
    out_stat,
    got_acc,
    got_stat,
    slot_of,
    base_of,
    res_sem,
    block_sems,
    acc_send,
    acc_recv,
    stat_send,
    stat_recv,
):
    seq_index = lax.axis_index("seq")
    head_index = lax.axis_index("head")
    senders = seq_count * head_count
    me = seq_index * head_count + head_index
    step_count, request_count, group_size, head_dim = queries.shape
    rows = step_count * group_size
    resident = res_kv.shape[1]
    res_rows = res_kv.shape[2]
    dev_blocks, block_len = prefill.shape[2], prefill.shape[3]
    slot_count = senders * dev_blocks // seq_count
    scale = 1.0 / math.sqrt(head_dim)
    joined = join_step[0]

    barrier = pltpu.get_barrier_semaphore()

    def greet(o, _):
        peer = lax.rem(me + o, senders)
        pl.semaphore_signal(
            barrier,
            inc=1,
            device_id={"seq": peer // head_count, "head": lax.rem(peer, head_count)},
            device_id_type=MESH,
        )
        return 0

    lax.fori_loop(1, senders, greet, 0)

    res_copies = []
    for r in range(resident):
        for c in range(2):
            copy = pltpu.make_async_copy(res_kv.at[c, r], res_buf.at[c, r], res_sem.at[c, r])
            copy.start()
            res_copies.append(copy)

    def block_for(sender, shard):
        found = jnp.int32(0)
        slot = jnp.int32(0)
        for k in range(dev_blocks):
            here = table[sender * dev_blocks + k]
            hit = (here // slot_count) == shard
            found = jnp.where(hit, k, found)
            slot = jnp.where(hit, here, slot)
        return found, slot

    def stage(z, _):
        found, _slot = block_for(me, z)
        for h in range(head_count):
            for c in range(2):
                staged[z * head_count + h, c] = prefill[c, h, found]
        return 0

    lax.fori_loop(0, seq_count, stage, 0)
    pl.semaphore_wait(barrier, senders - 1)

    def send(o, _):
        peer = lax.rem(me + o, senders)
        pltpu.make_async_remote_copy(
            src_ref=staged.at[peer],
            dst_ref=arrived.at[me],
            send_sem=block_sems.at[0],
            recv_sem=block_sems.at[1],
            device_id={"seq": peer // head_count, "head": lax.rem(peer, head_count)},
            device_id_type=MESH,
        ).start()
        return 0

    lax.fori_loop(1, senders, send, 0)
    arrived[me] = staged[me]

    def locate(s, _):
        found, slot = block_for(s, seq_index)
        slot_of[s] = slot - seq_index * slot_count
        base_of[s] = (s * dev_blocks + found) * block_len
        return 0

    lax.fori_loop(0, senders, locate, 0)

    def query_rows(r):
        wide = queries[:, r].astype(jnp.float32).reshape(rows, head_dim)
        return wide.astype(jnp.bfloat16)

    def fold(carry, keys, values, valid, q):
        m, l, acc = carry
        s = lax.dot_general(keys, q, NT, preferred_element_type=jnp.float32) * scale
        s = jnp.where(valid, s, very_low)
        top = jnp.maximum(m, jnp.max(s, axis=0, keepdims=True))
        w = jnp.where(valid, jnp.exp(s - top), 0.0)
        keep = jnp.exp(m - top)
        l = l * keep + jnp.sum(w, axis=0, keepdims=True)
        acc = acc * keep + lax.dot_general(
            values, w.astype(jnp.bfloat16), TN, preferred_element_type=jnp.float32
        )
        return top, l, acc

    empty = (
        jnp.full((1, rows), very_low, jnp.float32),
        jnp.zeros((1, rows), jnp.float32),
        jnp.zeros((head_dim, rows), jnp.float32),
    )

    chunk = math.gcd(res_rows, 1024)
    for r in range(resident):
        q = query_rows(r)
        res_copies[2 * r].wait()
        res_copies[2 * r + 1].wait()
        limit = lengths[r] - seq_index * res_rows

        def step(i, carry, r=r, q=q, limit=limit):
            at = pl.ds(pl.multiple_of(i * chunk, chunk), chunk)
            valid = lax.broadcasted_iota(jnp.int32, (chunk, rows), 0) + i * chunk < limit
            return fold(carry, res_buf[0, r, at], res_buf[1, r, at], valid, q)

        m, l, acc = lax.fori_loop(0, res_rows // chunk, step, empty)
        own_stat[2 * r : 2 * r + 1] = m
        own_stat[2 * r + 1 : 2 * r + 2] = l
        own_acc[r] = acc
        out_acc[r] = acc.astype(jnp.bfloat16)
        out_stat[0, 2 * r : 2 * r + 1] = m
        out_stat[0, 2 * r + 1 : 2 * r + 2] = l

    when = lax.broadcasted_iota(jnp.int32, (step_count, rows), 1) // group_size
    which = lax.broadcasted_iota(jnp.int32, (step_count, rows), 0)
    for r in range(request_count):
        allowed = which <= when
        if r >= resident:
            allowed = allowed & (which >= joined)
        m, l, acc = fold(empty, fresh[0, r], fresh[1, r], allowed, query_rows(r))
        fresh_stat[2 * r : 2 * r + 1] = m
        fresh_stat[2 * r + 1 : 2 * r + 2] = l
        fresh_acc[r] = acc

    def push(phase, first, count):
        for o in range(1, seq_count):
            peer = lax.rem(seq_index + o, seq_count)
            pltpu.make_async_remote_copy(
                src_ref=out_acc.at[pl.ds(first, count)],
                dst_ref=got_acc.at[seq_index, pl.ds(first, count)],
                send_sem=acc_send.at[phase],
                recv_sem=acc_recv.at[phase],
                device_id={"seq": peer},
                device_id_type=MESH,
            ).start()
            pltpu.make_async_remote_copy(
                src_ref=out_stat.at[phase],
                dst_ref=got_stat.at[seq_index, phase],
                send_sem=stat_send.at[phase],
                recv_sem=stat_recv.at[phase],
                device_id={"seq": peer},
                device_id_type=MESH,
            ).start()

    def drain(acc_sem, stat_sem, phase, first, count):
        part = got_acc.at[pl.ds(0, seq_count - 1), pl.ds(first, count)]
        pltpu.make_async_copy(part, part, acc_sem.at[phase]).wait()
        part = got_stat.at[pl.ds(0, seq_count - 1), phase]
        pltpu.make_async_copy(part, part, stat_sem.at[phase]).wait()

    push(0, 0, resident)

    part = arrived.at[pl.ds(0, senders - 1)]
    pltpu.make_async_copy(part, part, block_sems.at[1]).wait()

    q = query_rows(resident)
    some = math.gcd(senders, 16)

    def step(i, carry):
        first = i * some
        keys = arrived[pl.ds(first, some), 0].reshape(some * block_len, head_dim)
        values = arrived[pl.ds(first, some), 1].reshape(some * block_len, head_dim)
        offsets = lax.broadcasted_iota(jnp.int32, (block_len, rows), 0)
        positions = jnp.concatenate([offsets + base_of[first + s] for s in range(some)], axis=0)
        return fold(carry, keys, values, positions < lengths[resident], q)

    m, l, acc = lax.fori_loop(0, senders // some, step, empty)
    out_acc[resident] = acc.astype(jnp.bfloat16)
    out_stat[1, 0:1] = m
    out_stat[1, 1:2] = l
    own_stat[2 * resident : 2 * resident + 1] = m
    own_stat[2 * resident + 1 : 2 * resident + 2] = l
    own_acc[resident] = acc
    push(1, resident, 1)

    def place(j, _):
        def look(s, found):
            return jnp.where(slot_of[s] == j, s, found)

        source = lax.fori_loop(0, senders, look, jnp.int32(0), unroll=math.gcd(senders, 16))
        at = pl.ds(pl.multiple_of(j * block_len, block_len), block_len)
        for c in range(2):
            new_cache[c, 0, at] = arrived[source, c]
        return 0

    lax.fori_loop(0, slot_count, place, 0)

    def finish(r, phase, row):
        peers = [lax.rem(seq_index + o, seq_count) for o in range(1, seq_count)]
        maxima = [own_stat[2 * r : 2 * r + 1], fresh_stat[2 * r : 2 * r + 1]]
        totals = [own_stat[2 * r + 1 : 2 * r + 2], fresh_stat[2 * r + 1 : 2 * r + 2]]
        for peer in peers:
            maxima.append(got_stat[peer, phase, row : row + 1])
            totals.append(got_stat[peer, phase, row + 1 : row + 2])
        top = functools.reduce(jnp.maximum, maxima)
        factors = [jnp.exp(m - top) for m in maxima]
        total = sum(f * t for f, t in zip(factors, totals))
        summed = own_acc[r] * factors[0] + fresh_acc[r] * factors[1]
        for peer, f in zip(peers, factors[2:]):
            summed = summed + got_acc[peer, r].astype(jnp.float32) * f
        if r >= resident:
            lane = lax.broadcasted_iota(jnp.int32, (head_dim, rows), 1) // group_size
            summed = jnp.where(lane >= joined, summed / total, 0.0)
        else:
            summed = summed / total
        result = jnp.transpose(summed).reshape(step_count, group_size, head_dim)
        attn_out[:, r] = result.astype(jnp.bfloat16)

    drain(acc_recv, stat_recv, 0, 0, resident)
    for r in range(resident):
        finish(r, 0, 2 * r)
    drain(acc_recv, stat_recv, 1, resident, 1)
    finish(resident, 1, 0)

    part = staged.at[pl.ds(0, senders - 1)]
    pltpu.make_async_copy(part, part, block_sems.at[0]).wait()
    drain(acc_send, stat_send, 0, 0, resident)
    drain(acc_send, stat_send, 1, resident, 1)


def per_device(seq_count, head_count, queries, new_kv, res_kv, prefill_kv, block_table, lengths, join_step):
    step_count, request_count, group_size, head_dim = queries.shape
    rows = step_count * group_size
    resident, res_rows = res_kv.shape[1], res_kv.shape[2]
    head_total, new_rows = prefill_kv.shape[1], prefill_kv.shape[2]
    senders = seq_count * head_count
    dev_blocks = block_table.shape[0] // senders
    block_len = new_rows // dev_blocks
    if dev_blocks != seq_count or resident > 4 or head_total != head_count:
        raise ValueError("unsupported sizes")
    slot_count = block_table.shape[0] // seq_count
    fresh = jnp.transpose(new_kv[:, :, :, 0], (0, 2, 1, 3))
    prefill = prefill_kv.reshape(2, head_total, dev_blocks, block_len, head_dim)
    vmem = pl.BlockSpec(memory_space=pltpu.VMEM)
    smem = pl.BlockSpec(memory_space=pltpu.SMEM)
    bf16, f32 = jnp.bfloat16, jnp.float32
    return pl.pallas_call(
        functools.partial(kernel, seq_count, head_count),
        out_shape=(
            jax.ShapeDtypeStruct(queries.shape, bf16),
            jax.ShapeDtypeStruct((2, 1, slot_count * block_len, head_dim), bf16),
        ),
        in_specs=[vmem, vmem, vmem, smem, smem, smem, pl.BlockSpec(memory_space=pl.ANY)],
        out_specs=(vmem, vmem),
        scratch_shapes=[
            pltpu.VMEM((2, resident, res_rows, head_dim), bf16),
            pltpu.VMEM((senders, 2, block_len, head_dim), bf16),
            pltpu.VMEM((senders, 2, block_len, head_dim), bf16),
            pltpu.VMEM((request_count, head_dim, rows), f32),
            pltpu.VMEM((16, rows), f32),
            pltpu.VMEM((request_count, head_dim, rows), f32),
            pltpu.VMEM((16, rows), f32),
            pltpu.VMEM((request_count, head_dim, rows), bf16),
            pltpu.VMEM((2, 8, rows), f32),
            pltpu.VMEM((seq_count, request_count, head_dim, rows), bf16),
            pltpu.VMEM((seq_count, 2, 8, rows), f32),
            pltpu.SMEM((senders,), jnp.int32),
            pltpu.SMEM((senders,), jnp.int32),
            pltpu.SemaphoreType.DMA((2, resident)),
            pltpu.SemaphoreType.DMA((2,)),
            pltpu.SemaphoreType.DMA((2,)),
            pltpu.SemaphoreType.DMA((2,)),
            pltpu.SemaphoreType.DMA((2,)),
            pltpu.SemaphoreType.DMA((2,)),
        ],
        compiler_params=pltpu.CompilerParams(collective_id=0, has_side_effects=True),
    )(
        queries,
        fresh,
        prefill,
        block_table,
        lengths,
        join_step,
        res_kv.reshape(2, resident, res_rows, head_dim),
    )


def solution(mesh):
    in_specs = (
        P("groups", None, "head", None),
        P("groups", None, None, "head", None),
        P("groups", None, "seq", "head", None),
        P("groups", None, ("seq", "head"), None),
        P("groups"),
        P("groups"),
        P("groups"),
    )
    out_specs = (P("groups", None, "head", None), P("groups", "head", "seq", None))
    body = functools.partial(per_device, mesh.shape["seq"], mesh.shape["head"])
    return jax.shard_map(body, mesh=mesh, in_specs=in_specs, out_specs=out_specs, check_vma=False)
```

time: 73.3 us -> 34.8 us (0.47)
  blocking collectives: 41.9 us -> 0 us
  Pallas kernels: 0 us -> 29.9 us
  other arithmetic: 7.65 us -> 0 us
  starting transfers between devices: 7.39 us -> 0 us
  matrix products: 5.95 us -> 0 us
  local copies, waits for them, and re-layouts: 8.28 us -> 3.41 us
    all_gather x3 -> x0, blocking collectives: 41.9 us -> none  [merged_2(): everything = jax.tree.map(lambda part: lax.all_gather(part, axis), shard)]
    pallas_call x0 -> x1, Pallas kernels: none -> 29.9 us  [per_device(): pl.pallas_call(functools.partial(kernel, seq_count, head_count), out_shap...]
    all_to_all x1 -> x0, starting transfers between devices: 7.39 us -> none  [per_device(): lax.all_to_all(outgoing, ('seq', 'head'), split_axis=1, concat_axis=1, ti...]
    dot_general x8 -> x0, matrix products: 5.95 us -> none  [the longest x3 3.83 us: partial_softmax(): jnp.einsum('rd,pd->rp', query_rows, key_rows, preferred_element_type=jnp....]
    gather x5 -> x0, local copies, waits for them, and re-layouts: 2.65 us -> none  [the longest x2 0.68 us: per_device(): relaid = jnp.take(arrived, take_rows, axis=1)]
    reshape x8 -> x0, local copies, waits for them, and re-layouts: 2.11 us -> none  [the longest x2 0.87 us: per_device(): table_rows = block_table.reshape(senders, dev_blocks)]
    unnamed x13 -> x2, local copies, waits for them, and re-layouts: 1.38 us -> 3.41 us
    sort x3 -> x0, other arithmetic: 1.99 us -> none  [the longest x1 0.75 us: per_device(): send_order = jnp.argsort(own_slots)]
  transfers between devices with their start and end apart: 1 -> 0, of which waited for: 0 -> 0; matrix products, arithmetic and copies ran while one was open for 17% -> 0% of each run, Pallas kernels for 0% -> 0%
where the time goes in v1:
time: 34.8 us; the launch traced here: 34.6 us
  Pallas kernels  29.9 us (86%)
  local copies, waits for them, and re-layouts  3.41 us (10%)
  between operations  1.29 us (4%)
    pallas_call x1, Pallas kernels, per_device(): pl.pallas_call(functools.partial(kernel, seq_count, head_count), out_shap...  29.9 us
    unnamed x2, local copies, waits for them, and re-layouts  3.41 us

profile of v1, /device:TPU:0, one launch (start us, length us, event | category | flops | bytes accessed | tf_op | source)
XLA Modules:
  0.0 34.6 jit_solution(10586796286078959529)
XLA Ops:
  1.3 29.9 %shard_map.86 = (bf16[16,3,8,128]{3,2,1,0:T(8,128)(2,1)}, bf16[2,1,1024,128]{3,2,1,0:T(8,128)(2,1)}) custom-call(bf16[16,3,8,128]{3,2,1,0:T(8,128)(2,1)} %queries.1, bf16[2,3,16,128]{3,2,1,0:T(8,128)(2,1)} %bitcast.7, bf16[2,4,4,64,128]{4,3,2,1,0:T(8,128)(2,1)} %bitcast.6, s32[64]{0:T(128)} %table.1, s32[3]{0:T(128)} %lengths.1, s32[1]{0:T(128)S(6)} %copy.11.join_step, ...), custom_call_target="tpu_custom_call" | custom-call | tf_op jit(solution)/shard_map/pallas_call | solution.py:292
  31.1 1.5 %copy.12 = bf16[16,3,8,128]{3,2,1,0:T(8,128)(2,1)} copy(bf16[16,3,8,128]{3,2,1,0:T(8,128)(2,1)} %get-tuple-element.4) | data formatting | bytes 196608
  32.7 1.9 %copy.13 = bf16[2,1,1024,128]{3,2,1,0:T(8,128)(2,1)} copy(bf16[2,1,1024,128]{3,2,1,0:T(8,128)(2,1)} %get-tuple-element.5) | data formatting | bytes 1048576

commit v2 on v1

--- a/solution.py
+++ b/solution.py
@@ -19,13 +19,14 @@
     head_count,
     queries,
     fresh,
-    prefill,
+    prefill_kv,
     table,
     lengths,
     join_step,
     res_kv,
     attn_out,
     new_cache,
+    prefill,
     res_buf,
     staged,
     arrived,
@@ -37,14 +38,20 @@
     out_stat,
     got_acc,
     got_stat,
+    slice_send,
+    slice_got,
+    whole_out,
     slot_of,
     base_of,
+    prefill_sem,
     res_sem,
     block_sems,
     acc_send,
     acc_recv,
     stat_send,
     stat_recv,
+    slice_sems,
+    whole_sems,
 ):
     seq_index = lax.axis_index("seq")
     head_index = lax.axis_index("head")
@@ -58,7 +65,11 @@
     slot_count = senders * dev_blocks // seq_count
     scale = 1.0 / math.sqrt(head_dim)
     joined = join_step[0]
-
+    part_dim = head_dim // seq_count
+    peers = [lax.rem(seq_index + o, seq_count) for o in range(1, seq_count)]
+
+    fetch = pltpu.make_async_copy(prefill_kv, prefill, prefill_sem)
+    fetch.start()
     barrier = pltpu.get_barrier_semaphore()
 
     def greet(o, _):
@@ -97,6 +108,7 @@
                 staged[z * head_count + h, c] = prefill[c, h, found]
         return 0
 
+    fetch.wait()
     lax.fori_loop(0, seq_count, stage, 0)
     pl.semaphore_wait(barrier, senders - 1)
 
@@ -162,7 +174,9 @@
         own_stat[2 * r : 2 * r + 1] = m
         own_stat[2 * r + 1 : 2 * r + 2] = l
         own_acc[r] = acc
-        out_acc[r] = acc.astype(jnp.bfloat16)
+        pieces = acc.reshape(seq_count, part_dim, rows).astype(jnp.bfloat16)
+        for z in range(seq_count):
+            slice_send[z, r] = pieces[z]
         out_stat[0, 2 * r : 2 * r + 1] = m
         out_stat[0, 2 * r + 1 : 2 * r + 2] = l
 
@@ -177,33 +191,59 @@
         fresh_stat[2 * r + 1 : 2 * r + 2] = l
         fresh_acc[r] = acc
 
-    def push(phase, first, count):
-        for o in range(1, seq_count):
-            peer = lax.rem(seq_index + o, seq_count)
-            pltpu.make_async_remote_copy(
-                src_ref=out_acc.at[pl.ds(first, count)],
-                dst_ref=got_acc.at[seq_index, pl.ds(first, count)],
-                send_sem=acc_send.at[phase],
-                recv_sem=acc_recv.at[phase],
-                device_id={"seq": peer},
-                device_id_type=MESH,
-            ).start()
-            pltpu.make_async_remote_copy(
-                src_ref=out_stat.at[phase],
-                dst_ref=got_stat.at[seq_index, phase],
-                send_sem=stat_send.at[phase],
-                recv_sem=stat_recv.at[phase],
-                device_id={"seq": peer},
-                device_id_type=MESH,
-            ).start()
-
-    def drain(acc_sem, stat_sem, phase, first, count):
-        part = got_acc.at[pl.ds(0, seq_count - 1), pl.ds(first, count)]
-        pltpu.make_async_copy(part, part, acc_sem.at[phase]).wait()
-        part = got_stat.at[pl.ds(0, seq_count - 1), phase]
-        pltpu.make_async_copy(part, part, stat_sem.at[phase]).wait()
-
-    push(0, 0, resident)
+    def remote(source, target, send_sem, recv_sem, peer):
+        pltpu.make_async_remote_copy(
+            src_ref=source,
+            dst_ref=target,
+            send_sem=send_sem,
+            recv_sem=recv_sem,
+            device_id={"seq": peer},
+            device_id_type=MESH,
+        ).start()
+
+    def drain(buffer, sem):
+        part = buffer.at[pl.ds(0, seq_count - 1)]
+        pltpu.make_async_copy(part, part, sem).wait()
+
+    def push_stat(phase):
+        for peer in peers:
+            remote(
+                out_stat.at[phase],
+                got_stat.at[phase, seq_index],
+                stat_send.at[phase],
+                stat_recv.at[phase],
+                peer,
+            )
+
+    def merge(r, phase, row, own, new, got):
+        maxima = [own_stat[2 * r : 2 * r + 1], fresh_stat[2 * r : 2 * r + 1]]
+        totals = [own_stat[2 * r + 1 : 2 * r + 2], fresh_stat[2 * r + 1 : 2 * r + 2]]
+        for peer in peers:
+            maxima.append(got_stat[phase, peer, row : row + 1])
+            totals.append(got_stat[phase, peer, row + 1 : row + 2])
+        top = functools.reduce(jnp.maximum, maxima)
+        factors = [jnp.exp(m - top) for m in maxima]
+        total = sum(f * t for f, t in zip(factors, totals))
+        summed = own * factors[0] + new * factors[1]
+        for peer, f in zip(peers, factors[2:]):
+            summed = summed + got(peer).astype(jnp.float32) * f
+        return summed / total
+
+    push_stat(0)
+    for peer in peers:
+        remote(slice_send.at[peer], slice_got.at[seq_index], slice_sems.at[0], slice_sems.at[1], peer)
+
+    drain(got_stat.at[0], stat_recv.at[0])
+    drain(slice_got, slice_sems.at[1])
+    mine = pl.ds(pl.multiple_of(seq_index * part_dim, part_dim), part_dim)
+    for r in range(resident):
+        whole_out[seq_index, r] = merge(
+            r, 0, 2 * r, own_acc[r, mine], fresh_acc[r, mine], lambda peer: slice_got[peer, r]
+        ).astype(jnp.bfloat16)
+    for peer in peers:
+        remote(
+            whole_out.at[seq_index], whole_out.at[seq_index], whole_sems.at[0], whole_sems.at[1], peer
+        )
 
     part = arrived.at[pl.ds(0, senders - 1)]
     pltpu.make_async_copy(part, part, block_sems.at[1]).wait()
@@ -220,13 +260,15 @@
         return fold(carry, keys, values, positions < lengths[resident], q)
 
     m, l, acc = lax.fori_loop(0, senders // some, step, empty)
-    out_acc[resident] = acc.astype(jnp.bfloat16)
+    out_acc[...] = acc.astype(jnp.bfloat16)
     out_stat[1, 0:1] = m
     out_stat[1, 1:2] = l
     own_stat[2 * resident : 2 * resident + 1] = m
     own_stat[2 * resident + 1 : 2 * resident + 2] = l
     own_acc[resident] = acc
-    push(1, resident, 1)
+    push_stat(1)
+    for peer in peers:
+        remote(out_acc, got_acc.at[seq_index], acc_send, acc_recv, peer)
 
     def place(j, _):
         def look(s, found):
@@ -240,37 +282,28 @@
 
     lax.fori_loop(0, slot_count, place, 0)
 
-    def finish(r, phase, row):
-        peers = [lax.rem(seq_index + o, seq_count) for o in range(1, seq_count)]
-        maxima = [own_stat[2 * r : 2 * r + 1], fresh_stat[2 * r : 2 * r + 1]]
-        totals = [own_stat[2 * r + 1 : 2 * r + 2], fresh_stat[2 * r + 1 : 2 * r + 2]]
-        for peer in peers:
-            maxima.append(got_stat[peer, phase, row : row + 1])
-            totals.append(got_stat[peer, phase, row + 1 : row + 2])
-        top = functools.reduce(jnp.maximum, maxima)
-        factors = [jnp.exp(m - top) for m in maxima]
-        total = sum(f * t for f, t in zip(factors, totals))
-        summed = own_acc[r] * factors[0] + fresh_acc[r] * factors[1]
-        for peer, f in zip(peers, factors[2:]):
-            summed = summed + got_acc[peer, r].astype(jnp.float32) * f
-        if r >= resident:
-            lane = lax.broadcasted_iota(jnp.int32, (head_dim, rows), 1) // group_size
-            summed = jnp.where(lane >= joined, summed / total, 0.0)
-        else:
-            summed = summed / total
-        result = jnp.transpose(summed).reshape(step_count, group_size, head_dim)
+    def finish(r, result):
+        result = jnp.transpose(result).reshape(step_count, group_size, head_dim)
         attn_out[:, r] = result.astype(jnp.bfloat16)
 
-    drain(acc_recv, stat_recv, 0, 0, resident)
+    drain(whole_out, whole_sems.at[1])
     for r in range(resident):
-        finish(r, 0, 2 * r)
-    drain(acc_recv, stat_recv, 1, resident, 1)
-    finish(resident, 1, 0)
+        pieces = [whole_out[z, r].astype(jnp.float32) for z in range(seq_count)]
+        finish(r, jnp.concatenate(pieces, axis=0))
+    drain(got_stat.at[1], stat_recv.at[1])
+    drain(got_acc, acc_recv)
+    r = resident
+    result = merge(r, 1, 0, own_acc[r], fresh_acc[r], lambda peer: got_acc[peer])
+    lane = lax.broadcasted_iota(jnp.int32, (head_dim, rows), 1) // group_size
+    finish(r, jnp.where(lane >= joined, result, 0.0))
 
     part = staged.at[pl.ds(0, senders - 1)]
     pltpu.make_async_copy(part, part, block_sems.at[0]).wait()
-    drain(acc_send, stat_send, 0, 0, resident)
-    drain(acc_send, stat_send, 1, resident, 1)
+    drain(got_stat.at[0], stat_send.at[0])
+    drain(slice_got, slice_sems.at[0])
+    drain(whole_out, whole_sems.at[0])
+    drain(got_stat.at[1], stat_send.at[1])
+    drain(got_acc, acc_send)
 
 
 def per_device(seq_count, head_count, queries, new_kv, res_kv, prefill_kv, block_table, lengths, join_step):
@@ -286,18 +319,21 @@
     slot_count = block_table.shape[0] // seq_count
     fresh = jnp.transpose(new_kv[:, :, :, 0], (0, 2, 1, 3))
     prefill = prefill_kv.reshape(2, head_total, dev_blocks, block_len, head_dim)
+    part_dim = head_dim // seq_count
     vmem = pl.BlockSpec(memory_space=pltpu.VMEM)
     smem = pl.BlockSpec(memory_space=pltpu.SMEM)
+    hbm = pl.BlockSpec(memory_space=pltpu.HBM)
     bf16, f32 = jnp.bfloat16, jnp.float32
     return pl.pallas_call(
         functools.partial(kernel, seq_count, head_count),
         out_shape=(
-            jax.ShapeDtypeStruct(queries.shape, bf16),
-            jax.ShapeDtypeStruct((2, 1, slot_count * block_len, head_dim), bf16),
+            pltpu.VMEM(queries.shape, bf16),
+            pltpu.VMEM((2, 1, slot_count * block_len, head_dim), bf16),
         ),
-        in_specs=[vmem, vmem, vmem, smem, smem, smem, pl.BlockSpec(memory_space=pl.ANY)],
+        in_specs=[vmem, vmem, hbm, smem, smem, smem, hbm],
         out_specs=(vmem, vmem),
         scratch_shapes=[
+            pltpu.VMEM(prefill.shape, bf16),
             pltpu.VMEM((2, resident, res_rows, head_dim), bf16),
             pltpu.VMEM((senders, 2, block_len, head_dim), bf16),
             pltpu.VMEM((senders, 2, block_len, head_dim), bf16),
@@ -305,20 +341,28 @@
             pltpu.VMEM((16, rows), f32),
             pltpu.VMEM((request_count, head_dim, rows), f32),
             pltpu.VMEM((16, rows), f32),
-            pltpu.VMEM((request_count, head_dim, rows), bf16),
+            pltpu.VMEM((head_dim, rows), bf16),
             pltpu.VMEM((2, 8, rows), f32),
-            pltpu.VMEM((seq_count, request_count, head_dim, rows), bf16),
-            pltpu.VMEM((seq_count, 2, 8, rows), f32),
+            pltpu.VMEM((seq_count, head_dim, rows), bf16),
+            pltpu.VMEM((2, seq_count, 8, rows), f32),
+            pltpu.VMEM((seq_count, resident, part_dim, rows), bf16),
+            pltpu.VMEM((seq_count, resident, part_dim, rows), bf16),
+            pltpu.VMEM((seq_count, resident, part_dim, rows), bf16),
             pltpu.SMEM((senders,), jnp.int32),
             pltpu.SMEM((senders,), jnp.int32),
+            pltpu.SemaphoreType.DMA,
             pltpu.SemaphoreType.DMA((2, resident)),
             pltpu.SemaphoreType.DMA((2,)),
+            pltpu.SemaphoreType.DMA,
+            pltpu.SemaphoreType.DMA,
             pltpu.SemaphoreType.DMA((2,)),
             pltpu.SemaphoreType.DMA((2,)),
             pltpu.SemaphoreType.DMA((2,)),
             pltpu.SemaphoreType.DMA((2,)),
         ],
-        compiler_params=pltpu.CompilerParams(collective_id=0, has_side_effects=True),
+        compiler_params=pltpu.CompilerParams(
+            collective_id=0, has_side_effects=True, vmem_limit_bytes=48 * 1024 * 1024
+        ),
     )(
         queries,
         fresh,

time: 34.8 us -> 36.5 us (1.049)
  local copies, waits for them, and re-layouts: 3.41 us -> 7.6 us
  Pallas kernels: 29.9 us -> 27.3 us
    unnamed x2 -> x14, local copies, waits for them, and re-layouts: 3.41 us -> 7.6 us
    pallas_call x1, Pallas kernels: 29.9 us -> 27.3 us  [per_device(): pl.pallas_call(functools.partial(kernel, seq_count, head_count), out_shap...]
where the time goes in v2:
time: 36.5 us; the launch traced here: 36.2 us
  Pallas kernels  27.3 us (75%)
  local copies, waits for them, and re-layouts  7.6 us (21%)
  between operations  1.3 us (4%)
    pallas_call x1, Pallas kernels, per_device(): pl.pallas_call(functools.partial(kernel, seq_count, head_count), out_shap...  27.3 us
    unnamed x14, local copies, waits for them, and re-layouts  7.6 us

profile of v2, /device:TPU:0, one launch (start us, length us, event | category | flops | bytes accessed | tf_op | source)
XLA Modules:
  0.0 36.2 jit_solution(2202495439022961507)
XLA Ops:
  1.3 0.0 copy-start
  1.3 2.2 %copy-done = bf16[2,2,4096,1,128]{4,2,3,1,0:T(8,128)(2,1)S(1)} copy-done((bf16[2,2,4096,1,128]{4,2,3,1,0:T(8,128)(2,1)S(1)}, bf16[2,2,4096,1,128]{4,2,3,1,0:T(8,128)(2,1)}, u32[]{:S(2)}) %copy-start) | copy-done | bytes 4194328
  3.5 0.0 copy-start.1
  3.5 1.0 %copy-done.1 = bf16[2,4,256,128]{3,2,1,0:T(8,128)(2,1)S(1)} copy-done((bf16[2,4,256,128]{3,2,1,0:T(8,128)(2,1)S(1)}, bf16[2,4,256,128]{3,2,1,0:T(8,128)(2,1)}, u32[]{:S(2)}) %copy-start.1) | copy-done | bytes 524312
  4.5 0.0 copy-start.2
  4.5 0.9 %copy-done.2 = bf16[16,3,8,128]{3,2,1,0:T(8,128)(2,1)S(1)} copy-done((bf16[16,3,8,128]{3,2,1,0:T(8,128)(2,1)S(1)}, bf16[16,3,8,128]{3,2,1,0:T(8,128)(2,1)}, u32[]{:S(2)}) %copy-start.2) | copy-done | bytes 98328
  5.4 0.0 copy-start.3
  5.4 0.7 %copy-done.3 = bf16[2,16,3,1,128]{4,1,3,2,0:T(8,128)(2,1)S(1)} copy-done((bf16[2,16,3,1,128]{4,1,3,2,0:T(8,128)(2,1)S(1)}, bf16[2,16,3,1,128]{4,1,3,2,0:T(8,128)(2,1)}, u32[]{:S(2)}) %copy-start.3) | copy-done | bytes 24600
  6.1 0.0 copy-start.4
  6.1 0.7 %copy-done.4 = s32[64]{0:T(128)S(1)} copy-done((s32[64]{0:T(128)S(1)}, s32[64]{0:T(128)}, u32[]{:S(2)}) %copy-start.4) | copy-done | bytes 280
  6.8 0.0 copy-start.5
  6.8 0.7 %copy-done.5 = s32[3]{0:T(128)S(1)} copy-done((s32[3]{0:T(128)S(1)}, s32[3]{0:T(128)}, u32[]{:S(2)}) %copy-start.5) | copy-done | bytes 36
  7.5 27.3 %shard_map.86 = (bf16[16,3,8,128]{3,2,1,0:T(8,128)(2,1)S(1)}, bf16[2,1,1024,128]{3,2,1,0:T(8,128)(2,1)S(1)}) custom-call(bf16[16,3,8,128]{3,2,1,0:T(8,128)(2,1)S(1)} %copy-done.2, bf16[2,3,16,128]{3,2,1,0:T(8,128)(2,1)S(1)} %bitcast.7, bf16[2,4,4,64,128]{4,3,2,1,0:T(8,128)(2,1)S(1)} %bitcast.6, s32[64]{0:T(128)S(1)} %copy-done.4, s32[3]{0:T(128)S(1)} %copy-done.5, ...), custom_call_target="tpu_custom_call" | custom-call | tf_op jit(solution)/shard_map/pallas_call | solution.py:327
  34.8 0.6 %copy.11 = bf16[16,3,8,128]{3,2,1,0:T(8,128)(2,1)} copy(bf16[16,3,8,128]{3,2,1,0:T(8,128)(2,1)S(1)} %get-tuple-element.2) | data formatting | bytes 196608
  35.4 0.8 %copy.12 = bf16[2,1,1024,128]{3,2,1,0:T(8,128)(2,1)} copy(bf16[2,1,1024,128]{3,2,1,0:T(8,128)(2,1)S(1)} %get-tuple-element.3) | data formatting | bytes 1048576
Async XLA Ops:
  1.3 2.2 %copy-start = (bf16[2,2,4096,1,128]{4,2,3,1,0:T(8,128)(2,1)S(1)}, bf16[2,2,4096,1,128]{4,2,3,1,0:T(8,128)(2,1)}, u32[]{:S(2)}) copy-start(bf16[2,2,4096,1,128]{4,2,3,1,0:T(8,128)(2,1)} %param.9) | copy-start | bytes 12582916
  3.5 1.0 %copy-start.1 = (bf16[2,4,256,128]{3,2,1,0:T(8,128)(2,1)S(1)}, bf16[2,4,256,128]{3,2,1,0:T(8,128)(2,1)}, u32[]{:S(2)}) copy-start(bf16[2,4,256,128]{3,2,1,0:T(8,128)(2,1)} %param.10) | copy-start | bytes 1572868
  4.5 0.9 %copy-start.2 = (bf16[16,3,8,128]{3,2,1,0:T(8,128)(2,1)S(1)}, bf16[16,3,8,128]{3,2,1,0:T(8,128)(2,1)}, u32[]{:S(2)}) copy-start(bf16[16,3,8,128]{3,2,1,0:T(8,128)(2,1)} %queries.1) | copy-start | bytes 294916
  5.4 0.7 %copy-start.3 = (bf16[2,16,3,1,128]{4,1,3,2,0:T(8,128)(2,1)S(1)}, bf16[2,16,3,1,128]{4,1,3,2,0:T(8,128)(2,1)}, u32[]{:S(2)}) copy-start(bf16[2,16,3,1,128]{4,1,3,2,0:T(8,128)(2,1)} %param.8) | copy-start | bytes 73732
  6.1 0.7 %copy-start.4 = (s32[64]{0:T(128)S(1)}, s32[64]{0:T(128)}, u32[]{:S(2)}) copy-start(s32[64]{0:T(128)} %table.1) | copy-start | bytes 772
  6.8 0.7 %copy-start.5 = (s32[3]{0:T(128)S(1)}, s32[3]{0:T(128)}, u32[]{:S(2)}) copy-start(s32[3]{0:T(128)} %lengths.1) | copy-start | bytes 40

commit v3 on v2

--- a/solution.py
+++ b/solution.py
@@ -320,6 +320,7 @@
     fresh = jnp.transpose(new_kv[:, :, :, 0], (0, 2, 1, 3))
     prefill = prefill_kv.reshape(2, head_total, dev_blocks, block_len, head_dim)
     part_dim = head_dim // seq_count
+    out_bytes = 2 * (queries.size + 2 * slot_count * block_len * head_dim)
     vmem = pl.BlockSpec(memory_space=pltpu.VMEM)
     smem = pl.BlockSpec(memory_space=pltpu.SMEM)
     hbm = pl.BlockSpec(memory_space=pltpu.HBM)
@@ -361,7 +362,7 @@
             pltpu.SemaphoreType.DMA((2,)),
         ],
         compiler_params=pltpu.CompilerParams(
-            collective_id=0, has_side_effects=True, vmem_limit_bytes=48 * 1024 * 1024
+            collective_id=0, has_side_effects=True, vmem_limit_bytes=62 * 2**20 - 3 * out_bytes
         ),
     )(
         queries,

time: 36.5 us -> 30.5 us (0.84)
  local copies, waits for them, and re-layouts: 7.6 us -> 1.44 us
  Pallas kernels: 27.3 us -> 27.7 us
    unnamed x14 -> x2, local copies, waits for them, and re-layouts: 7.6 us -> 1.44 us
where the time goes in v3:
time: 30.5 us; the launch traced here: 30.4 us
  Pallas kernels  27.7 us (91%)
  local copies, waits for them, and re-layouts  1.44 us (5%)
  between operations  1.29 us (4%)
    pallas_call x1, Pallas kernels, per_device(): pl.pallas_call(functools.partial(kernel, seq_count, head_count), out_shap...  27.7 us
    unnamed x2, local copies, waits for them, and re-layouts  1.44 us

profile of v3, /device:TPU:0, one launch (start us, length us, event | category | flops | bytes accessed | tf_op | source)
XLA Modules:
  0.0 30.4 jit_solution(18360496006515488229)
XLA Ops:
  1.3 27.7 %shard_map.86 = (bf16[16,3,8,128]{3,2,1,0:T(8,128)(2,1)S(1)}, bf16[2,1,1024,128]{3,2,1,0:T(8,128)(2,1)S(1)}) custom-call(bf16[16,3,8,128]{3,2,1,0:T(8,128)(2,1)} %queries.1, bf16[2,3,16,128]{3,2,1,0:T(8,128)(2,1)} %bitcast.7, bf16[2,4,4,64,128]{4,3,2,1,0:T(8,128)(2,1)} %bitcast.6, s32[64]{0:T(128)} %table.1, s32[3]{0:T(128)} %lengths.1, ...), custom_call_target="tpu_custom_call" | custom-call | tf_op jit(solution)/shard_map/pallas_call | solution.py:328
  28.9 0.6 %copy.11 = bf16[16,3,8,128]{3,2,1,0:T(8,128)(2,1)} copy(bf16[16,3,8,128]{3,2,1,0:T(8,128)(2,1)S(1)} %get-tuple-element.2) | data formatting | bytes 196608
  29.6 0.8 %copy.12 = bf16[2,1,1024,128]{3,2,1,0:T(8,128)(2,1)} copy(bf16[2,1,1024,128]{3,2,1,0:T(8,128)(2,1)S(1)} %get-tuple-element.3) | data formatting | bytes 1048576
